TPU v7x, 8 devices: a whole 2x2x1 slice. The times are simulated.
8 devices in a mesh: dp: 1 (over z), tp: 2 (over y), ep: 4 (over x, core).
Axes of the slice: x: 2, y: 2, z: 1, core: 2. Of those that a mesh axis runs over, the one named last changes fastest.
Arguments:
- tokens: bfloat16 [2048, 2048], P(('dp', 'ep', 'tp'))
- expert_ids: int32 [2048, 6], P(('dp', 'ep', 'tp'))
- gates: float32 [2048, 6], P(('dp', 'ep', 'tp'))
- w_gate: bfloat16 [64, 2048, 1408], P('ep', None, 'tp')
- w_up: bfloat16 [64, 2048, 1408], P('ep', None, 'tp')
- w_down: bfloat16 [64, 1408, 2048], P('ep', 'tp')
Outputs:
- output: bfloat16 [2048, 2048], P(('dp', 'ep', 'tp'))
All inputs are finite; a program needn't handle non-finite values.
Results may differ from a plain program's by a relative error of at most 0.00123.
Values are sent between devices in bfloat16 or wider.
A program may use at most 1 GiB of HBM per device.

v0:
```python
import jax
import jax.numpy as jnp
from jax import lax
from jax.sharding import PartitionSpec as P


def solution(mesh):
    ep_size = mesh.shape["ep"]
    row_spec = P(("dp", "ep", "tp"), None)

    def local_layer(tokens, expert_ids, gates, w_gate, w_up, w_down):
        top_k = expert_ids.shape[1]
        local_experts = w_gate.shape[0]
        hidden = tokens.shape[1]
        all_tokens = lax.all_gather(tokens, ("ep", "tp"), tiled=True)
        all_ids = lax.all_gather(expert_ids, ("ep", "tp"), tiled=True)
        all_gates = lax.all_gather(gates, ("ep", "tp"), tiled=True)
        group_rows = all_tokens.shape[0]
        load = group_rows * top_k // (local_experts * ep_size)
        local_ids = all_ids.reshape(-1) - lax.axis_index("ep") * local_experts
        is_mine = (local_ids >= 0) & (local_ids < local_experts)
        sort_key = jnp.where(is_mine, local_ids, local_experts)
        order = jnp.argsort(sort_key, stable=True)[: local_experts * load].reshape(local_experts, load)
        row_index = order // top_k
        gate_disp = all_gates.reshape(-1)[order]
        x_disp = all_tokens[row_index]
        hidden_gate = jnp.einsum("ecd,edf->ecf", x_disp, w_gate, preferred_element_type=jnp.float32)
        hidden_up = jnp.einsum("ecd,edf->ecf", x_disp, w_up, preferred_element_type=jnp.float32)
        act_rows = (jax.nn.silu(hidden_gate) * hidden_up).astype(jnp.bfloat16)
        out_rows = jnp.einsum("ecf,efd->ecd", act_rows, w_down, preferred_element_type=jnp.float32)
        weighted = (out_rows * gate_disp[:, :, None]).reshape(-1, hidden)
        partial_sum = jax.ops.segment_sum(weighted, row_index.reshape(-1), num_segments=group_rows)
        own_rows = lax.psum_scatter(partial_sum, ("ep", "tp"), scatter_dimension=0, tiled=True)
        return own_rows.astype(jnp.bfloat16)

    return jax.shard_map(local_layer, mesh=mesh, in_specs=(row_spec, row_spec, row_spec, P("ep", None, "tp"), P("ep", None, "tp"), P("ep", "tp", None)), out_specs=row_spec, check_vma=False)
```

profile of v0, /device:TPU:0, one launch (start us, length us, event | category | flops | bytes accessed | tf_op | source)
XLA Modules:
  0.0 324.6 jit_solution(16668561178102182372)
XLA Ops:
  6.5 0.0 all-gather.2.cloned.1.call-start
  6.5 0.7 all-gather.2.cloned.1.call-update
  7.3 0.0 reduce-scatter.2.cloned.1.call-start
  7.3 14.2 %all_gather.11 = f32[2048,6]{0,1:T(8,128)S(1)} all-gather(f32[256,6]{0,1:T(8,128)} %param.8), channel_id=1, replica_groups=mesh['dp'=1,'tp'=2,'ep'=4] {'ep','tp'}, dimensions={0}, use_global_device_ids=true | all-gather | bytes 55296 | tf_op jit(solution)/shard_map/all_gather | solution.py:17
  21.5 0.4 copy.8
  21.9 0.7 reshape.142
  22.6 11.4 %all_gather.9 = s32[2048,6]{0,1:T(8,128)S(1)} all-gather(s32[256,6]{0,1:T(8,128)} %param.7), channel_id=1, replica_groups=mesh['dp'=1,'tp'=2,'ep'=4] {'ep','tp'}, dimensions={0}, use_global_device_ids=true | all-gather | bytes 55296 | tf_op jit(solution)/shard_map/all_gather | solution.py:16
  34.1 0.4 copy.7
  34.4 0.7 sub.19
  35.2 8.2 %sort.17 = (s32[12288]{0:T(1024)}, s32[12288]{0:T(1024)S(1)}) sort(s32[12288]{0:T(1024)S(1)} %and_select_fusion, s32[12288]{0:T(1024)S(1)} %iota.4), dimensions={0}, to_apply=%region_0.1 | sort | flops 172032 | bytes 196608 | tf_op jit(solution)/shard_map/jit(argsort)/sort | solution.py:23
  43.4 0.1 reshape.141
  43.5 0.1 reshape.146
  43.5 0.1 reshape.154
  43.6 17.6 %gather_fusion.1 = f32[3072]{0:T(1024)S(1)} fusion(f32[12288]{0:T(1024)S(1)} %reshape.142, s32[3072]{0:T(1024)S(1)} %broadcast_clamp_fusion), kind=kCustom, calls=%fused_computation.1 | custom fusion | bytes 36864 | tf_op jit(solution)/shard_map/gather | solution.py:25
  61.2 0.1 reshape.153
  61.3 0.0 all-gather.2.cloned.1.call-done
  61.3 28.3 %gather_fusion = bf16[3072,2048]{1,0:T(8,128)(2,1)} fusion(bf16[2048,2048]{1,0:T(8,128)(2,1)} %all-gather.2.cloned.1.call-done, s32[3072]{0:T(1024)S(1)} %broadcast_clamp_fusion.1), kind=kCustom, calls=%fused_computation | custom fusion | bytes 25178112 | tf_op jit(solution)/shard_map/gather | solution.py:26
  89.6 25.6 %fusion.9 = f32[16,192,704]{2,1,0:T(8,128)} fusion(bf16[16,192,2048]{2,1,0:T(8,128)(2,1)} %bitcast.16, bf16[16,2048,704]{1,2,0:T(8,128)(2,1)} %param.9), kind=kOutput, calls=%fused_computation.25 | convolution fusion | flops 8858370048 | bytes 67371008 | tf_op jit(solution)/shard_map/ecd,edf->ecf/dot_general | solution.py:27
  115.2 46.1 %broadcast_multiply_fusion = f32[16,192,2048]{2,1,0:T(8,128)} fusion(f32[16,192]{1,0:T(8,128)S(1)} %reshape.153, bf16[16,704,2048]{2,1,0:T(8,128)(2,1)} %param.11, f32[16,192,704]{2,1,0:T(8,128)} %fusion.9, bf16[16,192,2048]{2,1,0:T(8,128)(2,1)} %bitcast.17, bf16[16,2048,704]{1,2,0:T(8,128)(2,1)} %param.10), kind=kOutput, calls=%fused_computation.3 | convolution fusion | flops 17736007680 | bytes 138686464 | tf_op jit(solution)/shard_map/ecf,efd->ecd/dot_general | solution.py:30
  161.3 46.5 %scatter_custom_fusion = f32[2048,2048]{1,0:T(8,128)} fusion(s32[3072]{0:T(1024)S(1)} %get-tuple-element.8, f32[3072,2048]{1,0:T(8,128)} %bitcast.18, f32[]{:T(128)} %constant.10.clone.1), kind=kCustom, calls=%fused_computation.5 | custom fusion | flops 6291456 | bytes 16777728 | tf_op jit(solution)/shard_map/scatter-add | solution.py:32
  207.8 0.0 reduce-scatter.2.cloned.1.call-update
  207.8 107.2 %reduce-scatter.2.cloned.1.call-done = f32[256,2048]{1,0:T(8,128)} async-done(((f32[2048,2048]{1,0:T(8,128)}), f32[256,2048]{1,0:T(8,128)}) %reduce-scatter.2.cloned.1.call-update) | async-done | bytes 2097168 | tf_op jit(solution)/shard_map/reduce_scatter | solution.py:33
  315.1 2.7 convert_element_type.7
  (7 shorter events, 0.1 us)
Async XLA Ops:
  6.5 54.8 %all-gather.2.cloned.1.call-start = ((), (), s32[]{:S(2)}) async-start(), calls=%async_computation.1 | async-start | bytes 9437184 | tf_op jit(solution)/shard_map/all_gather | solution.py:15
  7.3 307.8 %reduce-scatter.2.cloned.1.call-start = ((), (), s32[]{:S(2)}) async-start(), calls=%async_computation.2 | async-start | bytes 18874368 | tf_op jit(solution)/shard_map/reduce_scatter | solution.py:33
Sparse Core Ops, SparseCore 0:
  9.1 52.0 all-gather.1
  208.0 107.0 reduce-scatter.1
where the time goes:
time: 325 us
  waiting for transfers between devices  108 us (33%)
  matrix products  71.7 us (22%)
  other arithmetic  57.5 us (18%)
  local copies, waits for them, and re-layouts  48.3 us (15%)
  blocking collectives  25.7 us (8%)
  between operations  13.5 us (4%)
    reduce_scatter x1, waiting for transfers between devices, local_layer(): lax.psum_scatter(partial_sum, ('ep', 'tp'), scatter_dimension=0, tiled=True)  107 us
    scatter-add x1, other arithmetic, local_layer(): jax.ops.segment_sum(weighted, row_index.reshape(-1), num_segments=group_r...  46.5 us
    dot_general x1, matrix products, local_layer(): jnp.einsum('ecf,efd->ecd', act_rows, w_down, preferred_element_type=jnp.f...  46.1 us
    gather x1, local copies, waits for them, and re-layouts, local_layer(): x_disp = all_tokens[row_index]  28.3 us
    dot_general x1, matrix products, local_layer(): jnp.einsum('ecd,edf->ecf', x_disp, w_gate, preferred_element_type=jnp.flo...  25.6 us
    gather x2, local copies, waits for them, and re-layouts, local_layer(): gate_disp = all_gates.reshape(-1)[order]  17.7 us
    all_gather x1, blocking collectives, local_layer(): all_gates = lax.all_gather(gates, ('ep', 'tp'), tiled=True)  14.2 us
    all_gather x1, blocking collectives, local_layer(): all_ids = lax.all_gather(expert_ids, ('ep', 'tp'), tiled=True)  11.4 us
  transfers between devices with their start and end apart: 2, of which 1 were waited for; matrix products, arithmetic and copies ran while one was open for 9% of the time, Pallas kernels for 0%

commit v1 on v0

v1 whole, which is shorter than its diff:
```python
import functools

import jax
import jax.numpy as jnp
from jax import lax
from jax.experimental import pallas as pl
from jax.experimental.pallas import tpu as pltpu
from jax.sharding import PartitionSpec as P

MESH = pl.DeviceIdType.MESH
F32 = jnp.float32
BF16 = jnp.bfloat16

ROWS = 256
HALF = ROWS // 2
NDEV = 8
TOPC = 3
COLS = 1024


def _dot(a, b):
    return jnp.dot(a, b, preferred_element_type=F32)


def _dot_t(a, b):
    return lax.dot_general(a, b, (((1,), (1,)), ((), ())), preferred_element_type=F32)


def _coords():
    ep = lax.axis_index("ep")
    tp = lax.axis_index("tp")
    x = ep // 2
    k = ep - 2 * x
    return ep, tp, x, k


def _remote(src, dst, ssem, rsem, ep, tp):
    return pltpu.make_async_remote_copy(
        src_ref=src, dst_ref=dst, send_sem=ssem, recv_sem=rsem,
        device_id={"ep": ep, "tp": tp}, device_id_type=MESH)


def dispatch_kernel(nbuf, tok_ref, meta_ref, wg_hbm, wu_hbm, h_hbm, cidx_ref, gk_ref,
                    rb, meta_all, x_ref, wg_buf, wu_buf, h_buf, rank_ref, rankg_ref,
                    wsem, hsem, tsend, trecv, msend, mrecv):
    experts, load = x_ref.shape[0], x_ref.shape[1]
    hidden = x_ref.shape[2]
    ff = wg_buf.shape[1]
    ep, tp, x, k = _coords()
    me = ep * 2 + tp
    sib = 2 * x + (1 - k)
    xn = 2 * (1 - x) + k
    yt = 1 - tp

    def weights(e, slot):
        return (pltpu.make_async_copy(wg_hbm.at[e], wg_buf.at[slot], wsem.at[0, slot]),
                pltpu.make_async_copy(wu_hbm.at[e], wu_buf.at[slot], wsem.at[1, slot]))

    for e in range(nbuf):
        for cp in weights(e, e):
            cp.start()

    others = []
    for step in range(1, NDEV):
        d = lax.rem(me + step, NDEV)
        others.append((d // 2, d % 2, step))
    barrier = pltpu.get_barrier_semaphore()
    for oe, ot, _ in others:
        pl.semaphore_signal(barrier, inc=1, device_id={"ep": oe, "tp": ot}, device_id_type=MESH)
    pl.semaphore_wait(barrier, NDEV - 1)

    metas = []
    for oe, ot, step in others:
        cp = _remote(meta_ref, meta_all.at[me], msend.at[step - 1], mrecv.at[step - 1], oe, ot)
        cp.start()
        metas.append(cp)

    top, bot = pl.ds(0, HALF), pl.ds(HALF, HALF)
    own = (tok_ref.at[top], tok_ref.at[bot])
    x0 = _remote(own[0], rb.at[1, top], tsend.at[0], trecv.at[1, 0], xn, tp)
    y1 = _remote(own[1], rb.at[1, bot], tsend.at[1], trecv.at[1, 1], ep, yt)
    x1 = _remote(own[1], rb.at[2, top], tsend.at[2], trecv.at[2, 0], xn, tp)
    y0 = _remote(own[0], rb.at[2, bot], tsend.at[3], trecv.at[2, 1], ep, yt)
    fy = _remote(rb.at[1, top], rb.at[3, top], tsend.at[4], trecv.at[3, 0], ep, yt)
    fx = _remote(rb.at[1, bot], rb.at[3, bot], tsend.at[5], trecv.at[3, 1], xn, tp)
    sibs = [_remote(tok_ref if g == 0 else rb.at[g], rb.at[4 + g], tsend.at[6 + g],
                    trecv.at[4 + g, 0], sib, tp) for g in range(4)]
    for cp in (x0, y1, x1, y0, sibs[0]):
        cp.start()

    meta_all[me] = meta_ref[...]
    for cp in metas:
        cp.wait_recv()
    row_i = lax.broadcasted_iota(jnp.int32, (ROWS, ROWS), 0)
    col_i = lax.broadcasted_iota(jnp.int32, (ROWS, ROWS), 1)
    before = jnp.where(row_i < col_i, 1.0, 0.0).astype(BF16)
    e_row = lax.broadcasted_iota(jnp.int32, (experts, ROWS), 0)
    lower = jnp.where(lax.broadcasted_iota(jnp.int32, (experts, experts), 1)
                      < lax.broadcasted_iota(jnp.int32, (experts, experts), 0), 1.0, 0.0).astype(BF16)
    e_global = (e_row + ep * experts).astype(F32)
    e_base = e_row.astype(F32) * float(load)
    base = jnp.zeros((experts, 1), F32)
    for b in range(NDEV):
        ind = jnp.zeros((experts, ROWS), F32)
        gate = jnp.zeros((experts, ROWS), F32)
        for j in range(6):
            hit = meta_all[b, j:j + 1, :] == e_global
            ind = jnp.where(hit, 1.0, ind)
            gate = jnp.where(hit, meta_all[b, 8 + j:9 + j, :], gate)
        ind16 = ind.astype(BF16)
        rank = _dot(ind16, before) + base
        base = base + jnp.sum(ind, axis=1, keepdims=True)
        pos = _dot(lower, ind16)
        rank_ref[b] = jnp.where(ind > 0.5, rank, -1.0)
        slot = e_base + rank
        for c in range(TOPC):
            sel = (ind > 0.5) & (pos == float(c))
            idx = jnp.sum(jnp.where(sel, slot, 0.0), axis=0, keepdims=True)
            cidx_ref[c:c + 1, b * ROWS:(b + 1) * ROWS] = idx.astype(jnp.int32)
            gk_ref[c:c + 1, b * ROWS:(b + 1) * ROWS] = jnp.sum(jnp.where(sel, gate, 0.0), axis=0, keepdims=True)
    for s in range(2):
        kk = k if s == 0 else 1 - k
        b_own = (2 * x + kk) * 2 + tp
        b_x = (2 * (1 - x) + kk) * 2 + tp
        b_y = (2 * x + kk) * 2 + yt
        b_d = (2 * (1 - x) + kk) * 2 + yt
        rankg_ref[4 * s] = rank_ref[b_own]
        rankg_ref[4 * s + 1, :, 0:HALF] = rank_ref[b_x, :, 0:HALF]
        rankg_ref[4 * s + 1, :, HALF:ROWS] = rank_ref[b_y, :, HALF:ROWS]
        rankg_ref[4 * s + 2, :, 0:HALF] = rank_ref[b_x, :, HALF:ROWS]
        rankg_ref[4 * s + 2, :, HALF:ROWS] = rank_ref[b_y, :, 0:HALF]
        rankg_ref[4 * s + 3] = rank_ref[b_d]

    def one_hot(q, e):
        want = lax.broadcasted_iota(jnp.int32, (load, ROWS), 0).astype(F32)
        return jnp.where(want == rankg_ref[q, pl.ds(e, 1), :], 1.0, 0.0).astype(BF16)

    def gather(e, g):
        oh0, oh1 = one_hot(g, e), one_hot(4 + g, e)
        for n in range(0, hidden, 512):
            cols = pl.ds(n, 512)
            left = tok_ref[:, cols] if g == 0 else rb[g, :, cols]
            got = (_dot(oh0, left) + _dot(oh1, rb[4 + g, :, cols])).astype(BF16)
            if g == 0:
                x_ref[e, :, cols] = got
            else:
                x_ref[e, :, cols] = x_ref[e, :, cols] + got

    def gather_all(g):
        def body(e, carry):
            gather(e, g)
            return carry
        lax.fori_loop(0, experts, body, 0)

    sibs[0].wait_recv()
    gather_all(0)
    x0.wait_recv()
    fy.start()
    y1.wait_recv()
    fx.start()
    sibs[1].start()
    sibs[1].wait_recv()
    gather_all(1)
    x1.wait_recv()
    y0.wait_recv()
    sibs[2].start()
    sibs[2].wait_recv()
    gather_all(2)
    fy.wait_recv()
    fx.wait_recv()
    sibs[3].start()
    sibs[3].wait_recv()

    def expert(e, carry):
        slot = lax.rem(e, nbuf)
        gather(e, 3)
        for cp in weights(e, slot):
            cp.wait()
        for n0, n1 in ((0, 256), (256, 512), (512, ff)):
            a = _dot_t(wg_buf[slot, n0:n1, :], x_ref[e])
            b = _dot_t(wu_buf[slot, n0:n1, :], x_ref[e])
            h_buf[e, :, n0:n1] = (a * jax.nn.sigmoid(a) * b).T.astype(BF16)
        pltpu.make_async_copy(h_buf.at[e], h_hbm.at[e], hsem.at[e]).start()

        @pl.when(e + nbuf < experts)
        def _():
            for cp in weights(e + nbuf, slot):
                cp.start()
        return carry

    lax.fori_loop(0, experts, expert, 0)
    for e in range(experts):
        pltpu.make_async_copy(h_buf.at[e], h_hbm.at[e], hsem.at[e]).wait()
    for cp in metas + [x0, y1, x1, y0, fy, fx] + sibs:
        cp.wait_send()


def return_kernel(nbuf, h_ref, wd_hbm, cidx_ref, gk_ref, out_ref,
                  wd_buf, o_ref, psib, pown, r0, r1, r2,
                  wsem, s0, v0, s1, v1, s2, v2):
    experts, load = h_ref.shape[0], h_ref.shape[1]
    ncol = wd_hbm.shape[2] // COLS
    ep, tp, x, k = _coords()
    sib = 2 * x + (1 - k)
    xn = 2 * (1 - x) + k
    yt = 1 - tp

    def weights(i, slot):
        c, e = i // experts, i % experts
        cols = pl.ds(pl.multiple_of(c * COLS, COLS), COLS)
        return pltpu.make_async_copy(wd_hbm.at[e, :, cols], wd_buf.at[slot], wsem.at[slot])

    for i in range(nbuf):
        weights(i, i).start()

    barrier = pltpu.get_barrier_semaphore()
    for oe, ot in ((sib, tp), (xn, tp), (ep, yt)):
        pl.semaphore_signal(barrier, inc=1, device_id={"ep": oe, "tp": ot}, device_id_type=MESH)
    pl.semaphore_wait(barrier, 3)

    def down(c):
        def body(e, carry):
            i = c * experts + e
            slot = lax.rem(i, nbuf)
            weights(i, slot).wait()
            for n in range(0, COLS, 256):
                o = _dot(h_ref[e], wd_buf[slot, :, n:n + 256])
                for j in range(2):
                    o_ref[pl.ds(e * load, load), n // 128 + j, :] = o[:, j * 128:(j + 1) * 128]

            @pl.when(i + nbuf < ncol * experts)
            def _():
                weights(i + nbuf, slot).start()
            return carry
        lax.fori_loop(0, experts, body, 0)

    unroll = 8

    def combine(dst, blk):
        def body(i, carry):
            for u in range(unroll):
                r = i * unroll + u
                t = blk * ROWS + r
                v = None
                for c in range(TOPC):
                    term = o_ref[cidx_ref[c, t]] * gk_ref[c, t]
                    v = term if v is None else v + term
                dst[pl.ds(pl.multiple_of(r * 8, 8), 8), :] = v
            return carry
        lax.fori_loop(0, ROWS // unroll, body, 0)

    tile = 256

    def add_into(dst, src, rows):
        def body(i, carry):
            at = pl.ds(pl.multiple_of(i * tile, tile), tile)
            dst[at, :] = dst[at, :] + src[at, :]
            return carry
        lax.fori_loop(0, rows // tile, body, 0)

    lo, hi = pl.ds(0, HALF * 8), pl.ds(HALF * 8, HALF * 8)

    def block(g, kk):
        xd = x if g < 2 else 1 - x
        yd = tp if g % 2 == 0 else 1 - tp
        return (2 * xd + kk) * 2 + yd

    stage0 = {(c, g): _remote(psib.at[c, g], r0.at[c, g], s0.at[c, g], v0.at[c, g], sib, tp)
              for c in range(ncol) for g in range(4)}
    stage1 = {}
    stage2 = {}
    for c in range(ncol):
        for d in range(2):
            stage1[c, 0, d] = _remote(pown.at[c, 2 + d, lo], r1.at[c, 0, d], s1.at[c, 0, d], v1.at[c, 0, d], xn, tp)
            stage1[c, 1, d] = _remote(pown.at[c, 1 + 2 * d, hi], r1.at[c, 1, d], s1.at[c, 1, d], v1.at[c, 1, d], ep, yt)
        stage2[c, 0] = _remote(pown.at[c, 1, lo], r2.at[c, 0], s2.at[c, 0], v2.at[c, 0], ep, yt)
        stage2[c, 1] = _remote(pown.at[c, 2, hi], r2.at[c, 1], s2.at[c, 1], v2.at[c, 1], xn, tp)

    def merge(c, g):
        combine(pown.at[c, g], block(g, k))
        stage0[c, g].wait_recv()
        add_into(pown.at[c, g], r0.at[c, g], ROWS * 8)

    for c in range(ncol):
        down(c)
        for g in (3, 2):
            combine(psib.at[c, g], block(g, 1 - k))
            stage0[c, g].start()
        merge(c, 3)
        stage1[c, 0, 1].start()
        stage1[c, 1, 1].start()
        combine(psib.at[c, 1], block(1, 1 - k))
        stage0[c, 1].start()
        merge(c, 2)
        stage1[c, 0, 0].start()
        combine(psib.at[c, 0], block(0, 1 - k))
        stage0[c, 0].start()
        merge(c, 1)
        stage1[c, 1, 0].start()
        merge(c, 0)
    for c in range(ncol):
        stage1[c, 0, 1].wait_recv()
        add_into(pown.at[c, 1, lo], r1.at[c, 0, 1], HALF * 8)
        stage2[c, 0].start()
        stage1[c, 1, 1].wait_recv()
        add_into(pown.at[c, 2, hi], r1.at[c, 1, 1], HALF * 8)
        stage2[c, 1].start()
    for c in range(ncol):
        for half in range(2):
            stage1[c, half, 0].wait_recv()
            add_into(pown.at[c, 0, lo if half == 0 else hi], r1.at[c, half, 0], HALF * 8)
    for c in range(ncol):
        for half in range(2):
            stage2[c, half].wait_recv()

            def body(i, carry, c=c, half=half):
                row = half * HALF + i * 16
                for j in range(8):
                    parts = []
                    for q in range(2):
                        at = (i * 16 + q * 8) * 8 + j
                        parts.append(pown[c, 0, pl.ds(half * HALF * 8 + at, 8, stride=8), :]
                                     + r2[c, half, pl.ds(at, 8, stride=8), :])
                    val = jnp.concatenate(parts, axis=0).astype(BF16)
                    out_ref[pl.ds(pl.multiple_of(row, 16), 16), c * COLS + j * 128:c * COLS + (j + 1) * 128] = val
                return carry
            lax.fori_loop(0, HALF // 16, body, 0)
    for cp in list(stage0.values()) + list(stage1.values()) + list(stage2.values()):
        cp.wait_send()


def solution(mesh):
    row_spec = P(("dp", "ep", "tp"), None)

    def local_layer(tokens, expert_ids, gates, w_gate, w_up, w_down):
        experts, hidden, ff = w_gate.shape
        load = ROWS * NDEV * expert_ids.shape[1] // (experts * 4)
        pad = ((0, 2), (0, 0))
        meta = jnp.concatenate([jnp.pad(expert_ids.astype(F32).T, pad), jnp.pad(gates.T, pad)], axis=0)
        nbuf = 4
        vm = pl.BlockSpec(memory_space=pltpu.VMEM)
        hbm = pl.BlockSpec(memory_space=pl.ANY)
        h, cidx, gk = pl.pallas_call(
            functools.partial(dispatch_kernel, nbuf),
            out_shape=(jax.ShapeDtypeStruct((experts, load, ff), BF16),
                       jax.ShapeDtypeStruct((TOPC, ROWS * NDEV), jnp.int32),
                       jax.ShapeDtypeStruct((TOPC, ROWS * NDEV), F32)),
            in_specs=[vm, vm, hbm, hbm],
            out_specs=(hbm, vm, vm),
            scratch_shapes=[
                pltpu.VMEM((8, ROWS, hidden), BF16),
                pltpu.VMEM((NDEV, 16, ROWS), F32),
                pltpu.VMEM((experts, load, hidden), BF16),
                pltpu.VMEM((nbuf, ff, hidden), BF16),
                pltpu.VMEM((nbuf, ff, hidden), BF16),
                pltpu.VMEM((experts, load, ff), BF16),
                pltpu.VMEM((NDEV, experts, ROWS), F32),
                pltpu.VMEM((8, experts, ROWS), F32),
                pltpu.SemaphoreType.DMA((2, nbuf)),
                pltpu.SemaphoreType.DMA((experts,)),
                pltpu.SemaphoreType.DMA((10,)),
                pltpu.SemaphoreType.DMA((8, 2)),
                pltpu.SemaphoreType.DMA((NDEV - 1,)),
                pltpu.SemaphoreType.DMA((NDEV - 1,)),
            ],
            compiler_params=pltpu.CompilerParams(collective_id=0, has_side_effects=True, vmem_limit_bytes=63 * 2**20),
            name="dispatch_up",
        )(tokens, meta, jnp.swapaxes(w_gate, 1, 2), jnp.swapaxes(w_up, 1, 2))

        nbuf2 = 6
        ncol = hidden // COLS
        sm = pl.BlockSpec(memory_space=pltpu.SMEM)
        return pl.pallas_call(
            functools.partial(return_kernel, nbuf2),
            out_shape=jax.ShapeDtypeStruct((ROWS, hidden), BF16),
            in_specs=[vm, hbm, sm, sm],
            out_specs=vm,
            scratch_shapes=[
                pltpu.VMEM((nbuf2, ff, COLS), BF16),
                pltpu.VMEM((experts * load, 8, 128), F32),
                pltpu.VMEM((ncol, 4, ROWS * 8, 128), F32),
                pltpu.VMEM((ncol, 4, ROWS * 8, 128), F32),
                pltpu.VMEM((ncol, 4, ROWS * 8, 128), F32),
                pltpu.VMEM((ncol, 2, 2, HALF * 8, 128), F32),
                pltpu.VMEM((ncol, 2, HALF * 8, 128), F32),
                pltpu.SemaphoreType.DMA((nbuf2,)),
                pltpu.SemaphoreType.DMA((ncol, 4)),
                pltpu.SemaphoreType.DMA((ncol, 4)),
                pltpu.SemaphoreType.DMA((ncol, 2, 2)),
                pltpu.SemaphoreType.DMA((ncol, 2, 2)),
                pltpu.SemaphoreType.DMA((ncol, 2)),
                pltpu.SemaphoreType.DMA((ncol, 2)),
            ],
            compiler_params=pltpu.CompilerParams(collective_id=1, has_side_effects=True, vmem_limit_bytes=63 * 2**20),
            name="down_return",
        )(h, w_down, cidx, gk)

    return jax.shard_map(local_layer, mesh=mesh, in_specs=(row_spec, row_spec, row_spec, P("ep", None, "tp"), P("ep", None, "tp"), P("ep", "tp", None)), out_specs=row_spec, check_vma=False)
```

time: 325 us -> 189 us (0.58)
  Pallas kernels: 0 us -> 184 us
  waiting for transfers between devices: 108 us -> 0 us
  matrix products: 71.7 us -> 0 us
  other arithmetic: 57.5 us -> 2 us
  local copies, waits for them, and re-layouts: 48.3 us -> 2.3 us
  blocking collectives: 25.7 us -> 0 us
  between operations: 13.5 us -> 0.02 us
    pallas_call x0 -> x2, Pallas kernels: none -> 184 us  [the longest x1 98.9 us: local_layer(): pl.pallas_call(functools.partial(return_kernel, nbuf2), out_shape=jax.Sha...]
    reduce_scatter x1 -> x0, waiting for transfers between devices: 107 us -> none  [local_layer(): lax.psum_scatter(partial_sum, ('ep', 'tp'), scatter_dimension=0, tiled=True)]
    dot_general x2 -> x0, matrix products: 71.7 us -> none  [the longest x1 46.1 us: local_layer(): jnp.einsum('ecf,efd->ecd', act_rows, w_down, preferred_element_type=jnp.f...]
    scatter-add x1 -> x0, other arithmetic: 46.5 us -> none  [local_layer(): jax.ops.segment_sum(weighted, row_index.reshape(-1), num_segments=group_r...]
    gather x3 -> x0, local copies, waits for them, and re-layouts: 46 us -> none  [the longest x1 28.3 us: local_layer(): x_disp = all_tokens[row_index]]
    all_gather x2 -> x0, blocking collectives: 25.7 us -> none  [the longest x1 14.2 us: local_layer(): all_gates = lax.all_gather(gates, ('ep', 'tp'), tiled=True)]
    sort x1 -> x0, other arithmetic: 8.2 us -> none  [local_layer(): jnp.argsort(sort_key, stable=True)[:local_experts * load]]
  transfers between devices with their start and end apart: 2 -> 0, of which waited for: 1 -> 0; matrix products, arithmetic and copies ran while one was open for 9% -> 0% of each run, Pallas kernels for 0% -> 0%
where the time goes in v1:
time: 189 us
  Pallas kernels  184 us (97%)
  local copies, waits for them, and re-layouts  2.3 us (1%)
  other arithmetic  2 us (1%)
    pallas_call x1, Pallas kernels, local_layer(): pl.pallas_call(functools.partial(return_kernel, nbuf2), out_shape=jax.Sha...  98.9 us
    pallas_call x1, Pallas kernels, local_layer(): pl.pallas_call(functools.partial(dispatch_kernel, nbuf), out_shape=(jax.S...  85.5 us

profile of v1, /device:TPU:0, one launch (start us, length us, event | category | flops | bytes accessed | tf_op | source)
XLA Modules:
  0.0 188.7 jit_solution(2677387767317406690)
XLA Ops:
  0.0 0.7 convert_bitcast_fusion
  0.7 1.3 select_maximum_fusion.meta_ref
  2.0 85.5 %dispatch_up.1 = (bf16[16,192,704]{2,1,0:T(8,128)(2,1)}, s32[3,2048]{1,0:T(4,128)}, f32[3,2048]{1,0:T(4,128)}) custom-call(bf16[256,2048]{1,0:T(8,128)(2,1)} %tok_ref.1, f32[16,256]{1,0:T(8,128)} %select_maximum_fusion.meta_ref, bf16[16,704,2048]{2,1,0:T(8,128)(2,1)} %bitcast.5, bf16[16,704,2048]{2,1,0:T(8,128)(2,1)} %bitcast.6), custom_call_target="tpu_custom_call" | custom-call | tf_op jit(solution)/shard_map/dispatch_up/pallas_call | solution.py:343
  87.5 98.9 %down_return.1 = bf16[256,2048]{1,0:T(8,128)(2,1)} custom-call(bf16[16,192,704]{2,1,0:T(8,128)(2,1)} %get-tuple-element.8.h_ref, bf16[16,704,2048]{2,1,0:T(8,128)(2,1)} %wd_hbm.1, s32[3,2048]{1,0:T(4,128)} %get-tuple-element.9.cidx_ref, f32[3,2048]{1,0:T(4,128)} %get-tuple-element.10.gk_ref), custom_call_target="tpu_custom_call" | custom-call | tf_op jit(solution)/shard_map/down_return/pallas_call | solution.py:373
  186.4 2.3 %copy.8 = bf16[256,2048]{1,0:T(8,128)(2,1)} copy(bf16[256,2048]{1,0:T(8,128)(2,1)} %down_return.1) | data formatting | bytes 2097152

commit v2 on v1

--- a/solution.py
+++ b/solution.py
@@ -40,9 +40,9 @@
         device_id={"ep": ep, "tp": tp}, device_id_type=MESH)
 
 
-def dispatch_kernel(nbuf, tok_ref, meta_ref, wg_hbm, wu_hbm, h_hbm, cidx_ref, gk_ref,
-                    rb, meta_all, x_ref, wg_buf, wu_buf, h_buf, rank_ref, rankg_ref,
-                    wsem, hsem, tsend, trecv, msend, mrecv):
+def dispatch_kernel(nbuf, tok_ref, ids_ref, gates_ref, wg_hbm, wu_hbm, h_hbm, cidx_ref, gk_ref,
+                    rb, ids_all, gates_all, x_ref, wg_buf, wu_buf, h_buf, rank_ref, rankg_ref,
+                    wsem, hsem, xsend, ysend, ssend, trecv, srecv, msend, mrecv):
     experts, load = x_ref.shape[0], x_ref.shape[1]
     hidden = x_ref.shape[2]
     ff = wg_buf.shape[1]
@@ -71,24 +71,46 @@
 
     metas = []
     for oe, ot, step in others:
-        cp = _remote(meta_ref, meta_all.at[me], msend.at[step - 1], mrecv.at[step - 1], oe, ot)
-        cp.start()
-        metas.append(cp)
-
-    top, bot = pl.ds(0, HALF), pl.ds(HALF, HALF)
-    own = (tok_ref.at[top], tok_ref.at[bot])
-    x0 = _remote(own[0], rb.at[1, top], tsend.at[0], trecv.at[1, 0], xn, tp)
-    y1 = _remote(own[1], rb.at[1, bot], tsend.at[1], trecv.at[1, 1], ep, yt)
-    x1 = _remote(own[1], rb.at[2, top], tsend.at[2], trecv.at[2, 0], xn, tp)
-    y0 = _remote(own[0], rb.at[2, bot], tsend.at[3], trecv.at[2, 1], ep, yt)
-    fy = _remote(rb.at[1, top], rb.at[3, top], tsend.at[4], trecv.at[3, 0], ep, yt)
-    fx = _remote(rb.at[1, bot], rb.at[3, bot], tsend.at[5], trecv.at[3, 1], xn, tp)
-    sibs = [_remote(tok_ref if g == 0 else rb.at[g], rb.at[4 + g], tsend.at[6 + g],
-                    trecv.at[4 + g, 0], sib, tp) for g in range(4)]
-    for cp in (x0, y1, x1, y0, sibs[0]):
-        cp.start()
-
-    meta_all[me] = meta_ref[...]
+        for which, (src, dst) in enumerate(((ids_ref, ids_all), (gates_ref, gates_all))):
+            cp = _remote(src, dst.at[me], msend.at[which, step - 1], mrecv.at[which, step - 1], oe, ot)
+            cp.start()
+            metas.append(cp)
+
+    rows = (pl.ds(0, HALF), pl.ds(HALF, HALF))
+    wide = hidden // 2
+    cols = (pl.ds(0, wide), pl.ds(wide, wide))
+    xs, ys, sibs = {}, {}, {}
+    for c in range(2):
+        for g in (1, 2):
+            part = rows[g - 1], rows[2 - g]
+            xs[g, c] = _remote(tok_ref.at[part[0], cols[c]], rb.at[g, rows[0], cols[c]],
+                               xsend.at[g - 1, c], trecv.at[g - 1, 0, c], xn, tp)
+            ys[g, c] = _remote(tok_ref.at[part[1], cols[c]], rb.at[g, rows[1], cols[c]],
+                               ysend.at[g - 1, c], trecv.at[g - 1, 1, c], ep, yt)
+        ys[3, c] = _remote(rb.at[1, rows[0], cols[c]], rb.at[3, rows[0], cols[c]],
+                           ysend.at[2, c], trecv.at[2, 0, c], ep, yt)
+        xs[3, c] = _remote(rb.at[1, rows[1], cols[c]], rb.at[3, rows[1], cols[c]],
+                           xsend.at[2, c], trecv.at[2, 1, c], xn, tp)
+        for g in (1, 2, 3):
+            sibs[g, c] = _remote(rb.at[g, :, cols[c]], rb.at[4 + g, :, cols[c]],
+                                 ssend.at[g, c], srecv.at[g, c], sib, tp)
+    sib_own = _remote(tok_ref, rb.at[4], ssend.at[0, 0], srecv.at[0, 0], sib, tp)
+    for g in (1, 2):
+        for c in range(2):
+            xs[g, c].start()
+            ys[g, c].start()
+    sib_own.start()
+
+    def arrived(g, c):
+        xs[g, c].wait_recv()
+        ys[g, c].wait_recv()
+        if g == 1:
+            ys[3, c].start()
+            xs[3, c].start()
+        sibs[g, c].start()
+
+    ids_all[me] = ids_ref[...]
+    gates_all[me] = gates_ref[...]
     for cp in metas:
         cp.wait_recv()
     row_i = lax.broadcasted_iota(jnp.int32, (ROWS, ROWS), 0)
@@ -97,16 +119,16 @@
     e_row = lax.broadcasted_iota(jnp.int32, (experts, ROWS), 0)
     lower = jnp.where(lax.broadcasted_iota(jnp.int32, (experts, experts), 1)
                       < lax.broadcasted_iota(jnp.int32, (experts, experts), 0), 1.0, 0.0).astype(BF16)
-    e_global = (e_row + ep * experts).astype(F32)
+    e_global = e_row + ep * experts
     e_base = e_row.astype(F32) * float(load)
     base = jnp.zeros((experts, 1), F32)
     for b in range(NDEV):
         ind = jnp.zeros((experts, ROWS), F32)
         gate = jnp.zeros((experts, ROWS), F32)
         for j in range(6):
-            hit = meta_all[b, j:j + 1, :] == e_global
+            hit = ids_all[b, j:j + 1, :] == e_global
             ind = jnp.where(hit, 1.0, ind)
-            gate = jnp.where(hit, meta_all[b, 8 + j:9 + j, :], gate)
+            gate = jnp.where(hit, gates_all[b, j:j + 1, :], gate)
         ind16 = ind.astype(BF16)
         rank = _dot(ind16, before) + base
         base = base + jnp.sum(ind, axis=1, keepdims=True)
@@ -116,8 +138,12 @@
         for c in range(TOPC):
             sel = (ind > 0.5) & (pos == float(c))
             idx = jnp.sum(jnp.where(sel, slot, 0.0), axis=0, keepdims=True)
-            cidx_ref[c:c + 1, b * ROWS:(b + 1) * ROWS] = idx.astype(jnp.int32)
-            gk_ref[c:c + 1, b * ROWS:(b + 1) * ROWS] = jnp.sum(jnp.where(sel, gate, 0.0), axis=0, keepdims=True)
+            idx = idx.astype(jnp.int32)
+            gk = jnp.sum(jnp.where(sel, gate, 0.0), axis=0, keepdims=True)
+            for q in range(ROWS // 128):
+                at = (c * NDEV + b) * (ROWS // 128) + q
+                cidx_ref[at:at + 1, :] = idx[:, q * 128:(q + 1) * 128]
+                gk_ref[at:at + 1, :] = gk[:, q * 128:(q + 1) * 128]
     for s in range(2):
         kk = k if s == 0 else 1 - k
         b_own = (2 * x + kk) * 2 + tp
@@ -135,45 +161,45 @@
         want = lax.broadcasted_iota(jnp.int32, (load, ROWS), 0).astype(F32)
         return jnp.where(want == rankg_ref[q, pl.ds(e, 1), :], 1.0, 0.0).astype(BF16)
 
-    def gather(e, g):
+    def gather(e, g, c):
         oh0, oh1 = one_hot(g, e), one_hot(4 + g, e)
-        for n in range(0, hidden, 512):
-            cols = pl.ds(n, 512)
-            left = tok_ref[:, cols] if g == 0 else rb[g, :, cols]
-            got = (_dot(oh0, left) + _dot(oh1, rb[4 + g, :, cols])).astype(BF16)
+        for n in range(c * wide, (c + 1) * wide, 512):
+            at = pl.ds(n, 512)
+            left = tok_ref[:, at] if g == 0 else rb[g, :, at]
+            got = (_dot(oh0, left) + _dot(oh1, rb[4 + g, :, at])).astype(BF16)
             if g == 0:
-                x_ref[e, :, cols] = got
+                x_ref[e, :, at] = got
             else:
-                x_ref[e, :, cols] = x_ref[e, :, cols] + got
-
-    def gather_all(g):
+                x_ref[e, :, at] = x_ref[e, :, at] + got
+
+    def gather_all(g, halves, hook_at=None, hook=None):
         def body(e, carry):
-            gather(e, g)
+            if hook is not None:
+                pl.when(e == hook_at)(hook)
+            for c in halves:
+                gather(e, g, c)
             return carry
         lax.fori_loop(0, experts, body, 0)
 
-    sibs[0].wait_recv()
-    gather_all(0)
-    x0.wait_recv()
-    fy.start()
-    y1.wait_recv()
-    fx.start()
-    sibs[1].start()
-    sibs[1].wait_recv()
-    gather_all(1)
-    x1.wait_recv()
-    y0.wait_recv()
-    sibs[2].start()
-    sibs[2].wait_recv()
-    gather_all(2)
-    fy.wait_recv()
-    fx.wait_recv()
-    sibs[3].start()
-    sibs[3].wait_recv()
+    sib_own.wait_recv()
+    gather_all(0, (0, 1), 8, lambda: arrived(1, 0))
+    arrived(1, 1)
+    sibs[1, 0].wait_recv()
+    gather_all(1, (0,))
+    arrived(2, 0)
+    sibs[1, 1].wait_recv()
+    gather_all(1, (1,))
+    sibs[2, 0].wait_recv()
+    gather_all(2, (0,), 3, lambda: arrived(2, 1))
+    sibs[2, 1].wait_recv()
+    gather_all(2, (1,), 8, lambda: arrived(3, 0))
+    sibs[3, 0].wait_recv()
+    gather_all(3, (0,), 12, lambda: arrived(3, 1))
+    sibs[3, 1].wait_recv()
 
     def expert(e, carry):
         slot = lax.rem(e, nbuf)
-        gather(e, 3)
+        gather(e, 3, 1)
         for cp in weights(e, slot):
             cp.wait()
         for n0, n1 in ((0, 256), (256, 512), (512, ff)):
@@ -191,13 +217,13 @@
     lax.fori_loop(0, experts, expert, 0)
     for e in range(experts):
         pltpu.make_async_copy(h_buf.at[e], h_hbm.at[e], hsem.at[e]).wait()
-    for cp in metas + [x0, y1, x1, y0, fy, fx] + sibs:
+    for cp in metas + list(xs.values()) + list(ys.values()) + list(sibs.values()) + [sib_own]:
         cp.wait_send()
 
 
-def return_kernel(nbuf, h_ref, wd_hbm, cidx_ref, gk_ref, out_ref,
-                  wd_buf, o_ref, psib, pown, r0, r1, r2,
-                  wsem, s0, v0, s1, v1, s2, v2):
+def return_kernel(nbuf, h_hbm, wd_hbm, cidx_hbm, gk_hbm, out_ref,
+                  cidx_ref, gk_ref, h_ref, wd_buf, o_ref, psib, pown, r0, r1, r2,
+                  hsem, wsem, s0, v0, s1, v1, s2, v2):
     experts, load = h_ref.shape[0], h_ref.shape[1]
     ncol = wd_hbm.shape[2] // COLS
     ep, tp, x, k = _coords()
@@ -210,13 +236,23 @@
         cols = pl.ds(pl.multiple_of(c * COLS, COLS), COLS)
         return pltpu.make_async_copy(wd_hbm.at[e, :, cols], wd_buf.at[slot], wsem.at[slot])
 
-    for i in range(nbuf):
+    ins = [pltpu.make_async_copy(h_hbm, h_ref, hsem.at[0]),
+           pltpu.make_async_copy(cidx_hbm, cidx_ref, hsem.at[1]),
+           pltpu.make_async_copy(gk_hbm, gk_ref, hsem.at[2])]
+    weights(0, 0).start()
+    for cp in ins:
+        cp.start()
+    for i in range(1, nbuf):
         weights(i, i).start()
 
     barrier = pltpu.get_barrier_semaphore()
     for oe, ot in ((sib, tp), (xn, tp), (ep, yt)):
         pl.semaphore_signal(barrier, inc=1, device_id={"ep": oe, "tp": ot}, device_id_type=MESH)
     pl.semaphore_wait(barrier, 3)
+    for cp in ins:
+        cp.wait()
+
+    o_lin = o_ref.reshape(experts * load * 8, 128)
 
     def down(c):
         def body(e, carry):
@@ -226,7 +262,8 @@
             for n in range(0, COLS, 256):
                 o = _dot(h_ref[e], wd_buf[slot, :, n:n + 256])
                 for j in range(2):
-                    o_ref[pl.ds(e * load, load), n // 128 + j, :] = o[:, j * 128:(j + 1) * 128]
+                    at = e * (load * 8) + (n // 128 + j)
+                    o_lin[pl.ds(at, load, stride=8), :] = o[:, j * 128:(j + 1) * 128]
 
             @pl.when(i + nbuf < ncol * experts)
             def _():
@@ -234,16 +271,16 @@
             return carry
         lax.fori_loop(0, experts, body, 0)
 
-    unroll = 8
+    unroll = 16
 
     def combine(dst, blk):
         def body(i, carry):
             for u in range(unroll):
                 r = i * unroll + u
-                t = blk * ROWS + r
                 v = None
                 for c in range(TOPC):
-                    term = o_ref[cidx_ref[c, t]] * gk_ref[c, t]
+                    t = (blk * ROWS + i * unroll) + (c * NDEV * ROWS + u)
+                    term = o_ref[cidx_ref[t]] * gk_ref[t]
                     v = term if v is None else v + term
                 dst[pl.ds(pl.multiple_of(r * 8, 8), 8), :] = v
             return carry
@@ -334,22 +371,22 @@
 
     def local_layer(tokens, expert_ids, gates, w_gate, w_up, w_down):
         experts, hidden, ff = w_gate.shape
-        load = ROWS * NDEV * expert_ids.shape[1] // (experts * 4)
-        pad = ((0, 2), (0, 0))
-        meta = jnp.concatenate([jnp.pad(expert_ids.astype(F32).T, pad), jnp.pad(gates.T, pad)], axis=0)
+        top_k = expert_ids.shape[1]
+        load = ROWS * NDEV * top_k // (experts * 4)
         nbuf = 4
         vm = pl.BlockSpec(memory_space=pltpu.VMEM)
         hbm = pl.BlockSpec(memory_space=pl.ANY)
         h, cidx, gk = pl.pallas_call(
             functools.partial(dispatch_kernel, nbuf),
             out_shape=(jax.ShapeDtypeStruct((experts, load, ff), BF16),
-                       jax.ShapeDtypeStruct((TOPC, ROWS * NDEV), jnp.int32),
-                       jax.ShapeDtypeStruct((TOPC, ROWS * NDEV), F32)),
-            in_specs=[vm, vm, hbm, hbm],
+                       jax.ShapeDtypeStruct((TOPC * ROWS * NDEV // 128, 128), jnp.int32),
+                       jax.ShapeDtypeStruct((TOPC * ROWS * NDEV // 128, 128), F32)),
+            in_specs=[vm, vm, vm, hbm, hbm],
             out_specs=(hbm, vm, vm),
             scratch_shapes=[
                 pltpu.VMEM((8, ROWS, hidden), BF16),
-                pltpu.VMEM((NDEV, 16, ROWS), F32),
+                pltpu.VMEM((NDEV, top_k, ROWS), jnp.int32),
+                pltpu.VMEM((NDEV, top_k, ROWS), F32),
                 pltpu.VMEM((experts, load, hidden), BF16),
                 pltpu.VMEM((nbuf, ff, hidden), BF16),
                 pltpu.VMEM((nbuf, ff, hidden), BF16),
@@ -358,24 +395,29 @@
                 pltpu.VMEM((8, experts, ROWS), F32),
                 pltpu.SemaphoreType.DMA((2, nbuf)),
                 pltpu.SemaphoreType.DMA((experts,)),
-                pltpu.SemaphoreType.DMA((10,)),
-                pltpu.SemaphoreType.DMA((8, 2)),
-                pltpu.SemaphoreType.DMA((NDEV - 1,)),
-                pltpu.SemaphoreType.DMA((NDEV - 1,)),
+                pltpu.SemaphoreType.DMA((3, 2)),
+                pltpu.SemaphoreType.DMA((3, 2)),
+                pltpu.SemaphoreType.DMA((4, 2)),
+                pltpu.SemaphoreType.DMA((3, 2, 2)),
+                pltpu.SemaphoreType.DMA((4, 2)),
+                pltpu.SemaphoreType.DMA((2, NDEV - 1)),
+                pltpu.SemaphoreType.DMA((2, NDEV - 1)),
             ],
             compiler_params=pltpu.CompilerParams(collective_id=0, has_side_effects=True, vmem_limit_bytes=63 * 2**20),
             name="dispatch_up",
-        )(tokens, meta, jnp.swapaxes(w_gate, 1, 2), jnp.swapaxes(w_up, 1, 2))
+        )(tokens, expert_ids.T, gates.T, jnp.swapaxes(w_gate, 1, 2), jnp.swapaxes(w_up, 1, 2))
 
         nbuf2 = 6
         ncol = hidden // COLS
-        sm = pl.BlockSpec(memory_space=pltpu.SMEM)
         return pl.pallas_call(
             functools.partial(return_kernel, nbuf2),
             out_shape=jax.ShapeDtypeStruct((ROWS, hidden), BF16),
-            in_specs=[vm, hbm, sm, sm],
+            in_specs=[hbm, hbm, hbm, hbm],
             out_specs=vm,
             scratch_shapes=[
+                pltpu.SMEM((TOPC * ROWS * NDEV,), jnp.int32),
+                pltpu.SMEM((TOPC * ROWS * NDEV,), F32),
+                pltpu.VMEM((experts, load, ff), BF16),
                 pltpu.VMEM((nbuf2, ff, COLS), BF16),
                 pltpu.VMEM((experts * load, 8, 128), F32),
                 pltpu.VMEM((ncol, 4, ROWS * 8, 128), F32),
@@ -383,6 +425,7 @@
                 pltpu.VMEM((ncol, 4, ROWS * 8, 128), F32),
                 pltpu.VMEM((ncol, 2, 2, HALF * 8, 128), F32),
                 pltpu.VMEM((ncol, 2, HALF * 8, 128), F32),
+                pltpu.SemaphoreType.DMA((3,)),
                 pltpu.SemaphoreType.DMA((nbuf2,)),
                 pltpu.SemaphoreType.DMA((ncol, 4)),
                 pltpu.SemaphoreType.DMA((ncol, 4)),
@@ -393,6 +436,6 @@
             ],
             compiler_params=pltpu.CompilerParams(collective_id=1, has_side_effects=True, vmem_limit_bytes=63 * 2**20),
             name="down_return",
-        )(h, w_down, cidx, gk)
+        )(h, w_down, cidx.reshape(-1), gk.reshape(-1))
 
     return jax.shard_map(local_layer, mesh=mesh, in_specs=(row_spec, row_spec, row_spec, P("ep", None, "tp"), P("ep", None, "tp"), P("ep", "tp", None)), out_specs=row_spec, check_vma=False)

time: 189 us -> 177 us (0.937)
  Pallas kernels: 184 us -> 175 us
  other arithmetic: 2 us -> 0 us
    pallas_call x1, Pallas kernels: 98.9 us -> 87 us  [local_layer(): pl.pallas_call(functools.partial(return_kernel, nbuf2), out_shape=jax.Sha...]
    pallas_call x1, Pallas kernels: 85.5 us -> 88 us  [local_layer(): pl.pallas_call(functools.partial(dispatch_kernel, nbuf), out_shape=(jax.S...]
where the time goes in v2:
time: 177 us
  Pallas kernels  175 us (99%)
  local copies, waits for them, and re-layouts  2.3 us (1%)
    pallas_call x1, Pallas kernels, local_layer(): pl.pallas_call(functools.partial(dispatch_kernel, nbuf), out_shape=(jax.S...  88 us
    pallas_call x1, Pallas kernels, local_layer(): pl.pallas_call(functools.partial(return_kernel, nbuf2), out_shape=jax.Sha...  87 us

profile of v2, /device:TPU:0, one launch (start us, length us, event | category | flops | bytes accessed | tf_op | source)
XLA Modules:
  0.0 177.3 jit_solution(3750619002010936187)
XLA Ops:
  0.0 88.0 %dispatch_up.1 = (bf16[16,192,704]{2,1,0:T(8,128)(2,1)}, s32[48,128]{1,0:T(8,128)}, f32[48,128]{1,0:T(8,128)}) custom-call(bf16[256,2048]{1,0:T(8,128)(2,1)} %tok_ref.1, s32[6,256]{1,0:T(8,128)} %bitcast.10, f32[6,256]{1,0:T(8,128)} %bitcast.11, bf16[16,704,2048]{2,1,0:T(8,128)(2,1)} %bitcast.6, bf16[16,704,2048]{2,1,0:T(8,128)(2,1)} %bitcast.7), custom_call_target="tpu_custom_call" | custom-call | tf_op jit(solution)/shard_map/dispatch_up/pallas_call | solution.py:379
  88.0 87.0 %down_return.1 = bf16[256,2048]{1,0:T(8,128)(2,1)} custom-call(bf16[16,192,704]{2,1,0:T(8,128)(2,1)} %get-tuple-element.8.h_hbm, bf16[16,704,2048]{2,1,0:T(8,128)(2,1)} %wd_hbm.1, s32[6144]{0:T(1024)} %bitcast.8, f32[6144]{0:T(1024)} %bitcast.9), custom_call_target="tpu_custom_call" | custom-call | tf_op jit(solution)/shard_map/down_return/pallas_call | solution.py:412
  175.0 2.3 %copy.8 = bf16[256,2048]{1,0:T(8,128)(2,1)} copy(bf16[256,2048]{1,0:T(8,128)(2,1)} %down_return.1) | data formatting | bytes 2097152

commit v3 on v2

--- a/solution.py
+++ b/solution.py
@@ -172,17 +172,20 @@
             else:
                 x_ref[e, :, at] = x_ref[e, :, at] + got
 
+    group = 4
+
     def gather_all(g, halves, hook_at=None, hook=None):
-        def body(e, carry):
+        def body(i, carry):
             if hook is not None:
-                pl.when(e == hook_at)(hook)
-            for c in halves:
-                gather(e, g, c)
+                pl.when(i == hook_at)(hook)
+            for u in range(group):
+                for c in halves:
+                    gather(i * group + u, g, c)
             return carry
-        lax.fori_loop(0, experts, body, 0)
+        lax.fori_loop(0, experts // group, body, 0)
 
     sib_own.wait_recv()
-    gather_all(0, (0, 1), 8, lambda: arrived(1, 0))
+    gather_all(0, (0, 1), 2, lambda: arrived(1, 0))
     arrived(1, 1)
     sibs[1, 0].wait_recv()
     gather_all(1, (0,))
@@ -190,31 +193,38 @@
     sibs[1, 1].wait_recv()
     gather_all(1, (1,))
     sibs[2, 0].wait_recv()
-    gather_all(2, (0,), 3, lambda: arrived(2, 1))
+    gather_all(2, (0,), 1, lambda: arrived(2, 1))
     sibs[2, 1].wait_recv()
-    gather_all(2, (1,), 8, lambda: arrived(3, 0))
+    gather_all(2, (1,), 2, lambda: arrived(3, 0))
     sibs[3, 0].wait_recv()
-    gather_all(3, (0,), 12, lambda: arrived(3, 1))
+    gather_all(3, (0,), 3, lambda: arrived(3, 1))
     sibs[3, 1].wait_recv()
 
-    def expert(e, carry):
-        slot = lax.rem(e, nbuf)
-        gather(e, 3, 1)
-        for cp in weights(e, slot):
-            cp.wait()
-        for n0, n1 in ((0, 256), (256, 512), (512, ff)):
-            a = _dot_t(wg_buf[slot, n0:n1, :], x_ref[e])
-            b = _dot_t(wu_buf[slot, n0:n1, :], x_ref[e])
-            h_buf[e, :, n0:n1] = (a * jax.nn.sigmoid(a) * b).T.astype(BF16)
-        pltpu.make_async_copy(h_buf.at[e], h_hbm.at[e], hsem.at[e]).start()
-
-        @pl.when(e + nbuf < experts)
+    pair = 2
+
+    def expert(i, carry):
+        ids = [i * pair + u for u in range(pair)]
+        for e in ids:
+            for cp in weights(e, lax.rem(e, nbuf)):
+                cp.wait()
+        for e in ids:
+            slot = lax.rem(e, nbuf)
+            gather(e, 3, 1)
+            for n0, n1 in ((0, 256), (256, 512), (512, ff)):
+                a = _dot_t(wg_buf[slot, n0:n1, :], x_ref[e])
+                b = _dot_t(wu_buf[slot, n0:n1, :], x_ref[e])
+                h_buf[e, :, n0:n1] = (a * jax.nn.sigmoid(a) * b).T.astype(BF16)
+        for e in ids:
+            pltpu.make_async_copy(h_buf.at[e], h_hbm.at[e], hsem.at[e]).start()
+
+        @pl.when(i * pair + nbuf < experts)
         def _():
-            for cp in weights(e + nbuf, slot):
-                cp.start()
+            for e in ids:
+                for cp in weights(e + nbuf, lax.rem(e, nbuf)):
+                    cp.start()
         return carry
 
-    lax.fori_loop(0, experts, expert, 0)
+    lax.fori_loop(0, experts // pair, expert, 0)
     for e in range(experts):
         pltpu.make_async_copy(h_buf.at[e], h_hbm.at[e], hsem.at[e]).wait()
     for cp in metas + list(xs.values()) + list(ys.values()) + list(sibs.values()) + [sib_own]:
@@ -255,21 +265,26 @@
     o_lin = o_ref.reshape(experts * load * 8, 128)
 
     def down(c):
-        def body(e, carry):
-            i = c * experts + e
-            slot = lax.rem(i, nbuf)
-            weights(i, slot).wait()
-            for n in range(0, COLS, 256):
-                o = _dot(h_ref[e], wd_buf[slot, :, n:n + 256])
-                for j in range(2):
-                    at = e * (load * 8) + (n // 128 + j)
-                    o_lin[pl.ds(at, load, stride=8), :] = o[:, j * 128:(j + 1) * 128]
-
-            @pl.when(i + nbuf < ncol * experts)
+        def body(p, carry):
+            ids = [p * 2 + u for u in range(2)]
+            for e in ids:
+                i = c * experts + e
+                weights(i, lax.rem(i, nbuf)).wait()
+            for e in ids:
+                slot = lax.rem(c * experts + e, nbuf)
+                for n in range(0, COLS, 256):
+                    o = _dot(h_ref[e], wd_buf[slot, :, n:n + 256])
+                    for j in range(2):
+                        at = e * (load * 8) + (n // 128 + j)
+                        o_lin[pl.ds(at, load, stride=8), :] = o[:, j * 128:(j + 1) * 128]
+
+            @pl.when(c * experts + p * 2 + nbuf < ncol * experts)
             def _():
-                weights(i + nbuf, slot).start()
+                for e in ids:
+                    i = c * experts + e
+                    weights(i + nbuf, lax.rem(i, nbuf)).start()
             return carry
-        lax.fori_loop(0, experts, body, 0)
+        lax.fori_loop(0, experts // 2, body, 0)
 
     unroll = 16
 
@@ -373,7 +388,7 @@
         experts, hidden, ff = w_gate.shape
         top_k = expert_ids.shape[1]
         load = ROWS * NDEV * top_k // (experts * 4)
-        nbuf = 4
+        nbuf = 6
         vm = pl.BlockSpec(memory_space=pltpu.VMEM)
         hbm = pl.BlockSpec(memory_space=pl.ANY)
         h, cidx, gk = pl.pallas_call(
@@ -407,7 +422,7 @@
             name="dispatch_up",
         )(tokens, expert_ids.T, gates.T, jnp.swapaxes(w_gate, 1, 2), jnp.swapaxes(w_up, 1, 2))
 
-        nbuf2 = 6
+        nbuf2 = 8
         ncol = hidden // COLS
         return pl.pallas_call(
             functools.partial(return_kernel, nbuf2),

time: 177 us -> 165 us (0.932)
  Pallas kernels: 175 us -> 162 us
    pallas_call x1, Pallas kernels: 88 us -> 75.4 us  [local_layer(): pl.pallas_call(functools.partial(dispatch_kernel, nbuf), out_shape=(jax.S...]
where the time goes in v3:
time: 165 us; the launch traced here: 164 us
  Pallas kernels  162 us (98%)
  local copies, waits for them, and re-layouts  2.3 us (1%)
    pallas_call x1, Pallas kernels, local_layer(): pl.pallas_call(functools.partial(return_kernel, nbuf2), out_shape=jax.Sha...  86.8 us
    pallas_call x1, Pallas kernels, local_layer(): pl.pallas_call(functools.partial(dispatch_kernel, nbuf), out_shape=(jax.S...  75.4 us

profile of v3, /device:TPU:0, one launch (start us, length us, event | category | flops | bytes accessed | tf_op | source)
XLA Modules:
  0.0 164.5 jit_solution(4840899236682287985)
XLA Ops:
  0.0 75.4 %dispatch_up.1 = (bf16[16,192,704]{2,1,0:T(8,128)(2,1)}, s32[48,128]{1,0:T(8,128)}, f32[48,128]{1,0:T(8,128)}) custom-call(bf16[256,2048]{1,0:T(8,128)(2,1)} %tok_ref.1, s32[6,256]{1,0:T(8,128)} %bitcast.10, f32[6,256]{1,0:T(8,128)} %bitcast.11, bf16[16,704,2048]{2,1,0:T(8,128)(2,1)} %bitcast.6, bf16[16,704,2048]{2,1,0:T(8,128)(2,1)} %bitcast.7), custom_call_target="tpu_custom_call" | custom-call | tf_op jit(solution)/shard_map/dispatch_up/pallas_call | solution.py:394
  75.4 86.8 %down_return.1 = bf16[256,2048]{1,0:T(8,128)(2,1)} custom-call(bf16[16,192,704]{2,1,0:T(8,128)(2,1)} %get-tuple-element.8.h_hbm, bf16[16,704,2048]{2,1,0:T(8,128)(2,1)} %wd_hbm.1, s32[6144]{0:T(1024)} %bitcast.8, f32[6144]{0:T(1024)} %bitcast.9), custom_call_target="tpu_custom_call" | custom-call | tf_op jit(solution)/shard_map/down_return/pallas_call | solution.py:427
  162.2 2.3 %copy.8 = bf16[256,2048]{1,0:T(8,128)(2,1)} copy(bf16[256,2048]{1,0:T(8,128)(2,1)} %down_return.1) | data formatting | bytes 2097152

commit v4 on v3

--- a/solution.py
+++ b/solution.py
@@ -41,7 +41,7 @@
 
 
 def dispatch_kernel(nbuf, tok_ref, ids_ref, gates_ref, wg_hbm, wu_hbm, h_hbm, cidx_ref, gk_ref,
-                    rb, ids_all, gates_all, x_ref, wg_buf, wu_buf, h_buf, rank_ref, rankg_ref,
+                    rb, ids_all, gates_all, x_ref, wg_buf, wu_buf, part_ref, h_buf, rank_ref, rankg_ref,
                     wsem, hsem, xsend, ysend, ssend, trecv, srecv, msend, mrecv):
     experts, load = x_ref.shape[0], x_ref.shape[1]
     hidden = x_ref.shape[2]
@@ -52,12 +52,15 @@
     xn = 2 * (1 - x) + k
     yt = 1 - tp
 
-    def weights(e, slot):
-        return (pltpu.make_async_copy(wg_hbm.at[e], wg_buf.at[slot], wsem.at[0, slot]),
-                pltpu.make_async_copy(wu_hbm.at[e], wu_buf.at[slot], wsem.at[1, slot]))
-
-    for e in range(nbuf):
-        for cp in weights(e, e):
+    wide = hidden // 2
+
+    def weights(i, slot):
+        e, at = i % experts, pl.ds(pl.multiple_of(i // experts * wide, wide), wide)
+        return (pltpu.make_async_copy(wg_hbm.at[e, :, at], wg_buf.at[slot], wsem.at[0, slot]),
+                pltpu.make_async_copy(wu_hbm.at[e, :, at], wu_buf.at[slot], wsem.at[1, slot]))
+
+    for i in range(nbuf):
+        for cp in weights(i, i):
             cp.start()
 
     others = []
@@ -77,7 +80,6 @@
             metas.append(cp)
 
     rows = (pl.ds(0, HALF), pl.ds(HALF, HALF))
-    wide = hidden // 2
     cols = (pl.ds(0, wide), pl.ds(wide, wide))
     xs, ys, sibs = {}, {}, {}
     for c in range(2):
@@ -96,9 +98,8 @@
                                  ssend.at[g, c], srecv.at[g, c], sib, tp)
     sib_own = _remote(tok_ref, rb.at[4], ssend.at[0, 0], srecv.at[0, 0], sib, tp)
     for g in (1, 2):
-        for c in range(2):
-            xs[g, c].start()
-            ys[g, c].start()
+        xs[g, 0].start()
+        ys[g, 0].start()
     sib_own.start()
 
     def arrived(g, c):
@@ -108,6 +109,10 @@
             ys[3, c].start()
             xs[3, c].start()
         sibs[g, c].start()
+        if (g, c) == (1, 0):
+            for q in (1, 2):
+                xs[q, 1].start()
+                ys[q, 1].start()
 
     ids_all[me] = ids_ref[...]
     gates_all[me] = gates_ref[...]
@@ -186,47 +191,67 @@
 
     sib_own.wait_recv()
     gather_all(0, (0, 1), 2, lambda: arrived(1, 0))
+    sibs[1, 0].wait_recv()
+    gather_all(1, (0,), 2, lambda: arrived(2, 0))
+    sibs[2, 0].wait_recv()
+    gather_all(2, (0,), 3, lambda: arrived(3, 0))
+    sibs[3, 0].wait_recv()
+    gather_all(3, (0,))
     arrived(1, 1)
-    sibs[1, 0].wait_recv()
-    gather_all(1, (0,))
-    arrived(2, 0)
-    sibs[1, 1].wait_recv()
-    gather_all(1, (1,))
-    sibs[2, 0].wait_recv()
-    gather_all(2, (0,), 1, lambda: arrived(2, 1))
-    sibs[2, 1].wait_recv()
-    gather_all(2, (1,), 2, lambda: arrived(3, 0))
-    sibs[3, 0].wait_recv()
-    gather_all(3, (0,), 3, lambda: arrived(3, 1))
-    sibs[3, 1].wait_recv()
 
     pair = 2
 
-    def expert(i, carry):
-        ids = [i * pair + u for u in range(pair)]
-        for e in ids:
-            for cp in weights(e, lax.rem(e, nbuf)):
-                cp.wait()
-        for e in ids:
-            slot = lax.rem(e, nbuf)
-            gather(e, 3, 1)
-            for n0, n1 in ((0, 256), (256, 512), (512, ff)):
-                a = _dot_t(wg_buf[slot, n0:n1, :], x_ref[e])
-                b = _dot_t(wu_buf[slot, n0:n1, :], x_ref[e])
-                h_buf[e, :, n0:n1] = (a * jax.nn.sigmoid(a) * b).T.astype(BF16)
-        for e in ids:
-            pltpu.make_async_copy(h_buf.at[e], h_hbm.at[e], hsem.at[e]).start()
-
-        @pl.when(i * pair + nbuf < experts)
-        def _():
-            for e in ids:
-                for cp in weights(e + nbuf, lax.rem(e, nbuf)):
-                    cp.start()
-        return carry
-
-    lax.fori_loop(0, experts // pair, expert, 0)
-    for e in range(experts):
-        pltpu.make_async_copy(h_buf.at[e], h_hbm.at[e], hsem.at[e]).wait()
+    def up_pass(c, hooks):
+        def body(j, carry):
+            for at, hook in hooks:
+                pl.when(j == at)(hook)
+            ids = [j * pair + u for u in range(pair)]
+            slots = [lax.rem(c * experts + e, nbuf) for e in ids]
+            for e, slot in zip(ids, slots):
+                for cp in weights(c * experts + e, slot):
+                    cp.wait()
+            if c == 1:
+                @pl.when(j * pair >= hslots)
+                def _():
+                    for e in ids:
+                        h_out(e - hslots).wait()
+            for e, slot in zip(ids, slots):
+                for n0, n1 in ((0, 256), (256, 512), (512, ff)):
+                    xe = x_ref[e, :, cols[c]]
+                    a = _dot_t(wg_buf[slot, n0:n1, :], xe)
+                    b = _dot_t(wu_buf[slot, n0:n1, :], xe)
+                    if c == 0:
+                        part_ref[0, e, n0:n1, :] = a
+                        part_ref[1, e, n0:n1, :] = b
+                    else:
+                        a = part_ref[0, e, n0:n1, :] + a
+                        b = part_ref[1, e, n0:n1, :] + b
+                        h_buf[lax.rem(e, hslots), :, n0:n1] = (a * jax.nn.sigmoid(a) * b).astype(BF16).T
+            if c == 1:
+                for e in ids:
+                    h_out(e).start()
+
+            @pl.when(c * experts + j * pair + nbuf < 2 * experts)
+            def _():
+                for e, slot in zip(ids, slots):
+                    for cp in weights(c * experts + e + nbuf, slot):
+                        cp.start()
+            return carry
+        lax.fori_loop(0, experts // pair, body, 0)
+
+    hslots = h_buf.shape[0]
+
+    def h_out(e):
+        slot = lax.rem(e, hslots)
+        return pltpu.make_async_copy(h_buf.at[slot], h_hbm.at[e], hsem.at[slot])
+
+    up_pass(0, ((3, lambda: arrived(2, 1)), (6, lambda: arrived(3, 1))))
+    for g in (1, 2, 3):
+        sibs[g, 1].wait_recv()
+        gather_all(g, (1,))
+    up_pass(1, ())
+    for e in range(experts - hslots, experts):
+        h_out(e).wait()
     for cp in metas + list(xs.values()) + list(ys.values()) + list(sibs.values()) + [sib_own]:
         cp.wait_send()
 
@@ -288,7 +313,7 @@
 
     unroll = 16
 
-    def combine(dst, blk):
+    def combine(dst, blk, first=0, count=ROWS):
         def body(i, carry):
             for u in range(unroll):
                 r = i * unroll + u
@@ -299,7 +324,7 @@
                     v = term if v is None else v + term
                 dst[pl.ds(pl.multiple_of(r * 8, 8), 8), :] = v
             return carry
-        lax.fori_loop(0, ROWS // unroll, body, 0)
+        lax.fori_loop(first // unroll, (first + count) // unroll, body, 0)
 
     tile = 256
 
@@ -317,8 +342,13 @@
         yd = tp if g % 2 == 0 else 1 - tp
         return (2 * xd + kk) * 2 + yd
 
+    halves = (lo, hi)
     stage0 = {(c, g): _remote(psib.at[c, g], r0.at[c, g], s0.at[c, g], v0.at[c, g], sib, tp)
-              for c in range(ncol) for g in range(4)}
+              for c in range(ncol) for g in range(3)}
+    for c in range(ncol):
+        for half in range(2):
+            at = halves[half]
+            stage0[c, 3, half] = _remote(psib.at[c, 3, at], r0.at[c, 3, at], s0.at[c, 3 + half], v0.at[c, 3 + half], sib, tp)
     stage1 = {}
     stage2 = {}
     for c in range(ncol):
@@ -335,12 +365,16 @@
 
     for c in range(ncol):
         down(c)
-        for g in (3, 2):
-            combine(psib.at[c, g], block(g, 1 - k))
-            stage0[c, g].start()
-        merge(c, 3)
-        stage1[c, 0, 1].start()
-        stage1[c, 1, 1].start()
+        for half in range(2):
+            combine(psib.at[c, 3], block(3, 1 - k), half * HALF, HALF)
+            stage0[c, 3, half].start()
+        for half in range(2):
+            combine(pown.at[c, 3], block(3, k), half * HALF, HALF)
+            stage0[c, 3, half].wait_recv()
+            add_into(pown.at[c, 3, halves[half]], r0.at[c, 3, halves[half]], HALF * 8)
+            stage1[c, half, 1].start()
+        combine(psib.at[c, 2], block(2, 1 - k))
+        stage0[c, 2].start()
         combine(psib.at[c, 1], block(1, 1 - k))
         stage0[c, 1].start()
         merge(c, 2)
@@ -403,13 +437,14 @@
                 pltpu.VMEM((NDEV, top_k, ROWS), jnp.int32),
                 pltpu.VMEM((NDEV, top_k, ROWS), F32),
                 pltpu.VMEM((experts, load, hidden), BF16),
-                pltpu.VMEM((nbuf, ff, hidden), BF16),
-                pltpu.VMEM((nbuf, ff, hidden), BF16),
-                pltpu.VMEM((experts, load, ff), BF16),
+                pltpu.VMEM((nbuf, ff, hidden // 2), BF16),
+                pltpu.VMEM((nbuf, ff, hidden // 2), BF16),
+                pltpu.VMEM((2, experts, ff, load), F32),
+                pltpu.VMEM((4, load, ff), BF16),
                 pltpu.VMEM((NDEV, experts, ROWS), F32),
                 pltpu.VMEM((8, experts, ROWS), F32),
                 pltpu.SemaphoreType.DMA((2, nbuf)),
-                pltpu.SemaphoreType.DMA((experts,)),
+                pltpu.SemaphoreType.DMA((4,)),
                 pltpu.SemaphoreType.DMA((3, 2)),
                 pltpu.SemaphoreType.DMA((3, 2)),
                 pltpu.SemaphoreType.DMA((4, 2)),
@@ -442,8 +477,8 @@
                 pltpu.VMEM((ncol, 2, HALF * 8, 128), F32),
                 pltpu.SemaphoreType.DMA((3,)),
                 pltpu.SemaphoreType.DMA((nbuf2,)),
-                pltpu.SemaphoreType.DMA((ncol, 4)),
-                pltpu.SemaphoreType.DMA((ncol, 4)),
+                pltpu.SemaphoreType.DMA((ncol, 5)),
+                pltpu.SemaphoreType.DMA((ncol, 5)),
                 pltpu.SemaphoreType.DMA((ncol, 2, 2)),
                 pltpu.SemaphoreType.DMA((ncol, 2, 2)),
                 pltpu.SemaphoreType.DMA((ncol, 2)),

time: 165 us -> 162 us (0.982)
  Pallas kernels: 162 us -> 160 us
where the time goes in v4:
time: 162 us
  Pallas kernels  160 us (99%)
  local copies, waits for them, and re-layouts  2.3 us (1%)
    pallas_call x1, Pallas kernels, local_layer(): pl.pallas_call(functools.partial(return_kernel, nbuf2), out_shape=jax.Sha...  85.8 us
    pallas_call x1, Pallas kernels, local_layer(): pl.pallas_call(functools.partial(dispatch_kernel, nbuf), out_shape=(jax.S...  74.1 us

profile of v4, /device:TPU:0, one launch (start us, length us, event | category | flops | bytes accessed | tf_op | source)
XLA Modules:
  0.0 162.2 jit_solution(17876611470869672853)
XLA Ops:
  0.0 74.1 %dispatch_up.1 = (bf16[16,192,704]{2,1,0:T(8,128)(2,1)}, s32[48,128]{1,0:T(8,128)}, f32[48,128]{1,0:T(8,128)}) custom-call(bf16[256,2048]{1,0:T(8,128)(2,1)} %tok_ref.1, s32[6,256]{1,0:T(8,128)} %bitcast.10, f32[6,256]{1,0:T(8,128)} %bitcast.11, bf16[16,704,2048]{2,1,0:T(8,128)(2,1)} %bitcast.6, bf16[16,704,2048]{2,1,0:T(8,128)(2,1)} %bitcast.7), custom_call_target="tpu_custom_call" | custom-call | tf_op jit(solution)/shard_map/dispatch_up/pallas_call | solution.py:428
  74.1 85.8 %down_return.1 = bf16[256,2048]{1,0:T(8,128)(2,1)} custom-call(bf16[16,192,704]{2,1,0:T(8,128)(2,1)} %get-tuple-element.8.h_hbm, bf16[16,704,2048]{2,1,0:T(8,128)(2,1)} %wd_hbm.1, s32[6144]{0:T(1024)} %bitcast.8, f32[6144]{0:T(1024)} %bitcast.9), custom_call_target="tpu_custom_call" | custom-call | tf_op jit(solution)/shard_map/down_return/pallas_call | solution.py:462
  159.9 2.3 %copy.8 = bf16[256,2048]{1,0:T(8,128)(2,1)} copy(bf16[256,2048]{1,0:T(8,128)(2,1)} %down_return.1) | data formatting | bytes 2097152
